TPU v7x, 32 devices: a whole 2x2x4 slice. The times are simulated.
32 devices in a mesh: dom: 8 (over z, y), edge: 4 (over x, core).
Axes of the slice: x: 2, y: 2, z: 4, core: 2. Of those that a mesh axis runs over, the one named last changes fastest.
Arguments:
- fine_nodes: bfloat16 [65536, 128], P('dom'), may hold values from -6 to 6
- fine_edges: bfloat16 [131072, 128], P(('dom', 'edge')), may hold values from -6 to 6
- fine_senders: int32 [131072], P(('dom', 'edge')), may hold values from 0 to 8703, as said below
- fine_receivers: int32 [131072], P(('dom', 'edge')), may hold values from 0 to 8191
- fine_halo: int32 [8, 8, 64], P('dom'), may hold values from 0 to 8191
- coarse_edges: bfloat16 [32768, 128], P(('dom', 'edge')), may hold values from -6 to 6
- coarse_senders: int32 [32768], P(('dom', 'edge')), may hold values from 0 to 2303, as said below
- coarse_receivers: int32 [32768], P(('dom', 'edge')), may hold values from 0 to 2047
- coarse_halo: int32 [8, 8, 32], P('dom'), may hold values from 0 to 2047
- pool_send: int32 [8, 8, 1536], P('dom'), may hold values from 0 to 8191, as said below
- pool_dest: int32 [8, 8, 1536], P('dom'), may hold values from 0 to 2048, as said below
- unpool_slot: int32 [65536], P('dom'), may hold values from 0 to 12287, as said below
- edge_in_weight: bfloat16 [2, 384, 128], replicated, may hold values from -0.3125 to 0.3125
- edge_out_weight: bfloat16 [2, 128, 128], replicated, may hold values from -0.5 to 0.5
- node_in_weight: bfloat16 [2, 256, 128], replicated, may hold values from -0.375 to 0.375
- node_out_weight: bfloat16 [2, 128, 128], replicated, may hold values from -0.5 to 0.5
- edge_gain: float32 [2, 128], replicated, may hold values from 0.5 to 1.5
- node_gain: float32 [2, 128], replicated, may hold values from 0.5 to 1.5
Outputs:
- fine_out: bfloat16 [65536, 128], P('dom')
- coarse_out: bfloat16 [16384, 128], P('dom')
Inputs may be any that keep to these rules, and one draw needn't show every extreme that they name: `fine_senders`: an entry below 8192 is a row of the edge's own partition; an entry 8192 + d * 64 + s names slot s of fine_halo[d, p] for the edge's partition p. `coarse_senders`: an entry below 2048 is a row of the edge's own coarse partition; an entry 2048 + d * 32 + s names slot s of coarse_halo[d, p]. pool_send[d, p, s] is a row of partition d. For each pair (d, p) the slots that carry data come first and number at most 1536; in every draw some p receives 1536 from every d. Every row of partition d is carried exactly once over all p and s; empty slots hold 0. pool_dest[p, d, s] is 2048 exactly where slot s of pool_send[d, p] is empty, else a row of coarse partition p. `unpool_slot`: row r of partition d holds p * 1536 + s for the one carrying slot with pool_send[d, p, s] = r.
All inputs are finite; a program needn't handle non-finite values.
Results may differ from a plain program's by a relative error of at most 0.0068.
Values may be sent and summed in bfloat16 or wider, within the bound.
No kernel may reach another device: no remote copies, remote signals or barrier semaphores. Data moves between devices by JAX's collectives and lax.ppermute only.
A program may use at most 64 MiB of HBM per device.

v0:
```python
import jax
import jax.numpy as jnp
from jax import lax
from jax.sharding import PartitionSpec as P

COARSE = 2048


def layer_norm(values, gain):
    center = values - jnp.mean(values, axis=-1, keepdims=True)
    spread = jnp.mean(center * center, axis=-1, keepdims=True)
    return center * lax.rsqrt(spread + 1e-05) * gain


def node_update(rows, summed, w_first, w_second, gain):
    inputs = jnp.concatenate([rows, summed.astype(jnp.bfloat16)], axis=1)
    hidden = jax.nn.silu(jnp.dot(inputs, w_first, preferred_element_type=jnp.float32)).astype(
        jnp.bfloat16
    )
    result = layer_norm(jnp.dot(hidden, w_second, preferred_element_type=jnp.float32), gain)
    return (rows.astype(jnp.float32) + result).astype(jnp.bfloat16)


def graph_layer(nodes, edges, senders, receivers, border, level, weights):
    edge_in_weight, edge_out_weight, node_in_weight, node_out_weight, edge_gain, node_gain = weights
    width = nodes.shape[-1]
    outgoing = nodes[border[0]]
    ghosts = lax.all_to_all(outgoing, "dom", split_axis=0, concat_axis=0, tiled=True)
    table = jnp.concatenate([nodes, ghosts.reshape(-1, width)], axis=0)
    inputs = jnp.concatenate([table[senders], nodes[receivers], edges], axis=1)
    hidden = jax.nn.silu(
        jnp.dot(inputs, edge_in_weight[level], preferred_element_type=jnp.float32)
    ).astype(jnp.bfloat16)
    message = layer_norm(
        jnp.dot(hidden, edge_out_weight[level], preferred_element_type=jnp.float32),
        edge_gain[level],
    )
    partial_sum = jax.ops.segment_sum(message, receivers, num_segments=nodes.shape[0])
    summed = lax.psum(partial_sum, "edge")
    return node_update(
        nodes, summed, node_in_weight[level], node_out_weight[level], node_gain[level]
    )


def pooled_mean(arrived, places, width):
    sums = jax.ops.segment_sum(
        arrived.reshape(-1, width).astype(jnp.float32), places, num_segments=COARSE + 1
    )[:COARSE]
    counts = jax.ops.segment_sum(jnp.ones_like(places), places, num_segments=COARSE + 1)[:COARSE]
    return (sums / jnp.maximum(counts, 1).astype(jnp.float32)[:, None]).astype(jnp.bfloat16)


def shards(
    fine_nodes,
    fine_edges,
    fine_senders,
    fine_receivers,
    fine_halo,
    coarse_edges,
    coarse_senders,
    coarse_receivers,
    coarse_halo,
    pool_send,
    pool_dest,
    unpool_slot,
    edge_in_weight,
    edge_out_weight,
    node_in_weight,
    node_out_weight,
    edge_gain,
    node_gain,
):
    weights = (
        edge_in_weight,
        edge_out_weight,
        node_in_weight,
        node_out_weight,
        edge_gain,
        node_gain,
    )
    width = fine_nodes.shape[-1]
    fine_mid = graph_layer(
        fine_nodes, fine_edges, fine_senders, fine_receivers, fine_halo, 0, weights
    )
    places = pool_dest[0].reshape(-1)
    arrived = lax.all_to_all(fine_mid[pool_send[0]], "dom", split_axis=0, concat_axis=0, tiled=True)
    coarse_in = pooled_mean(arrived, places, width)
    coarse_out = graph_layer(
        coarse_in, coarse_edges, coarse_senders, coarse_receivers, coarse_halo, 1, weights
    )
    padded = jnp.concatenate([coarse_out, jnp.zeros((1, width), jnp.bfloat16)], axis=0)
    back = lax.all_to_all(padded[pool_dest[0]], "dom", split_axis=0, concat_axis=0, tiled=True)
    parents = back.reshape(-1, width)[unpool_slot]
    fine_out = (fine_mid.astype(jnp.float32) + parents.astype(jnp.float32)).astype(jnp.bfloat16)
    return (fine_out, coarse_out)


def solution(mesh):
    placed = (
        P("dom", None),
        P(("dom", "edge"), None),
        P(("dom", "edge")),
        P(("dom", "edge")),
        P("dom", None, None),
        P(("dom", "edge"), None),
        P(("dom", "edge")),
        P(("dom", "edge")),
        P("dom", None, None),
        P("dom", None, None),
        P("dom", None, None),
        P("dom"),
        P(),
        P(),
        P(),
        P(),
        P(),
        P(),
    )
    return jax.shard_map(
        shards,
        mesh=mesh,
        in_specs=placed,
        out_specs=(P("dom", None), P("dom", None)),
        check_vma=False,
    )
```

profile of v0, /device:TPU:0, one launch (start us, length us, event | category | flops | bytes accessed | tf_op | source)
XLA Modules:
  0.0 604.5 jit_solution(17450261135767377777)
XLA Ops:
  0.6 0.7 compare_select_fusion.8
  1.4 3.5 gather_fusion
  4.9 7.3 %all-to-all-start = ((bf16[8,64,128]{2,1,0:T(8,128)(2,1)}), bf16[8,64,128]{2,1,0:T(8,128)(2,1)S(1)}, u32[]{:S(2)}, u32[]{:S(2)}) async-start(bf16[8,64,128]{2,1,0:T(8,128)(2,1)} %bitcast.1), calls=%async_computation | async-start | bytes 262144 | tf_op jit(solution)/shard_map/all_to_all | solution.py:28
  12.2 0.7 fusion.77
  13.0 0.8 slice_bitcast_fusion.1
  13.7 1.0 compare_select_fusion.1
  14.7 0.8 slice_bitcast_fusion
  15.5 4.1 copy.24
  19.5 12.1 %gather_fusion.2 = bf16[4096,128]{1,0:T(8,128)(2,1)S(1)} fusion(bf16[8192,128]{1,0:T(8,128)(2,1)S(1)} %copy-done, s32[4096]{0:T(1024)S(1)} %fusion.77), kind=kCustom, calls=%fused_computation.2 | custom fusion | bytes 2113536 | tf_op jit(solution)/shard_map/gather | solution.py:30
  31.7 5.6 pad_maximum_fusion
  37.3 16.2 %gather_fusion.1 = bf16[4096,128]{1,0:T(8,128)(2,1)} fusion(bf16[8704,128]{1,0:T(8,128)(2,1)} %pad_maximum_fusion, s32[4096]{0:T(1024)S(1)} %fusion.76), kind=kCustom, calls=%fused_computation.1 | custom fusion | bytes 2113536 | tf_op jit(solution)/shard_map/gather | solution.py:30
  53.5 4.3 fusion.95
  57.8 2.0 multiply_reduce_fusion.1
  59.8 0.2 copy-done.4
  60.0 1.7 multiply_multiply_fusion
  61.7 2.9 copy.25
  64.6 24.8 %scatter_custom_fusion = f32[8192,128]{1,0:T(8,128)} fusion(s32[4096]{0:T(1024)} %param.21, f32[4096,128]{1,0:T(8,128)} %copy.25, f32[]{:T(128)} %constant.13.clone.1), kind=kCustom, calls=%fused_computation.33 | custom fusion | flops 524288 | bytes 4194816 | tf_op jit(solution)/shard_map/scatter-add | solution.py:38
  89.4 77.1 %all-reduce.3 = bf16[8192,128]{1,0:T(8,128)(2,1)} all-reduce(f32[8192,128]{1,0:T(8,128)} %scatter_custom_fusion), channel_id=1, replica_groups=mesh['dom'=8,'edge'=4] {'edge'}, use_global_device_ids=true, to_apply=%region_3.4 | all-reduce | flops 1048576 | bytes 6291456 | tf_op jit(solution)/shard_map/psum | solution.py:39
  166.5 5.8 fusion.100
  172.3 2.8 multiply_reduce_fusion
  175.1 0.6 copy-done.2
  175.7 3.8 add_convert_fusion.1
  179.5 3.2 copy.26
  182.7 43.3 %gather_fusion.3 = bf16[12288,128]{1,0:T(8,128)(2,1)} fusion(bf16[8192,128]{1,0:T(8,128)(2,1)S(1)} %copy.26, s32[12288]{0:T(1024)S(1)} %broadcast_clamp_fusion.1), kind=kCustom, calls=%fused_computation.3 | custom fusion | bytes 6340608 | tf_op jit(solution)/shard_map/gather | solution.py:86
  226.0 5.5 all-to-all-start.1
  231.7 75.2 %scatter_custom_fusion.2 = s32[2049]{0:T(1024)S(1)} fusion(s32[12288]{0:T(1024)S(1)} %reshape.263, s32[12288]{0:T(1024)S(1)} %broadcast.163, s32[]{:T(128)} %constant.14.clone.1), kind=kCustom, calls=%fused_computation.101 | custom fusion | flops 12288 | bytes 8200 | tf_op jit(solution)/shard_map/scatter-add | solution.py:49
  307.1 76.8 %scatter_custom_fusion.1 = f32[2049,128]{1,0:T(8,128)} fusion(s32[12288]{0:T(1024)S(1)} %reshape.263, bf16[12288,128]{1,0:T(8,128)(2,1)S(1)} %bitcast.78, f32[]{:T(128)} %constant.13.clone.1), kind=kCustom, calls=%fused_computation.13 | custom fusion | flops 3145728 | bytes 4194820 | tf_op jit(solution)/shard_map/scatter-add | solution.py:46
  383.8 1.6 fusion.24
  385.4 1.5 gather_fusion.4
  386.8 11.6 %all-to-all-start.2 = ((bf16[8,32,128]{2,1,0:T(8,128)(2,1)}), bf16[8,32,128]{2,1,0:T(8,128)(2,1)S(1)}, u32[]{:S(2)}, u32[]{:S(2)}) async-start(bf16[8,32,128]{2,1,0:T(8,128)(2,1)} %bitcast.13), calls=%async_computation.2 | async-start | bytes 131072 | tf_op jit(solution)/shard_map/all_to_all | solution.py:28
  398.5 3.2 gather_fusion.6
  401.8 3.6 all-to-all-done.2
  405.4 3.2 gather_fusion.5
  408.7 0.6 fusion.105
  409.5 0.2 copy.27
  409.7 6.3 %scatter_custom_fusion.3 = f32[2048,128]{1,0:T(8,128)S(1)} fusion(s32[1024]{0:T(1024)S(1)} %copy-done.11, f32[1024,128]{1,0:T(8,128)S(1)} %copy.27, f32[]{:T(128)} %constant.13.clone.1), kind=kCustom, calls=%fused_computation.61 | custom fusion | flops 131072 | bytes 1048580 | tf_op jit(solution)/shard_map/scatter-add | solution.py:38
  416.0 25.8 %all-reduce.4 = bf16[2048,128]{1,0:T(8,128)(2,1)S(1)} all-reduce(f32[2048,128]{1,0:T(8,128)S(1)} %scatter_custom_fusion.3), channel_id=1, replica_groups=mesh['dom'=8,'edge'=4] {'edge'}, use_global_device_ids=true, to_apply=%region_11.12 | all-reduce | flops 262144 | bytes 1572864 | tf_op jit(solution)/shard_map/psum | solution.py:39
  441.8 0.9 fusion.110
  442.7 0.6 multiply_reduce_fusion.2
  443.3 1.0 add_convert_fusion.2
  444.3 0.8 copy-done.5
  445.2 43.3 %gather_fusion.7 = bf16[12288,128]{1,0:T(8,128)(2,1)} fusion(bf16[2049,128]{1,0:T(8,128)(2,1)S(1)} %concatenate.27, s32[12288]{0:T(1024)S(1)} %broadcast_clamp_fusion), kind=kCustom, calls=%fused_computation.7 | custom fusion | bytes 6340608 | tf_op jit(solution)/shard_map/gather | solution.py:92
  488.5 3.8 all-to-all-start.3
  492.3 71.3 %all-to-all-done.3 = bf16[8,1536,128]{2,1,0:T(8,128)(2,1)S(1)} async-done(((bf16[8,1536,128]{2,1,0:T(8,128)(2,1)}), bf16[8,1536,128]{2,1,0:T(8,128)(2,1)S(1)}, u32[]{:S(2)}, u32[]{:S(2)}) %all-to-all-start.3) | async-done | bytes 3145760 | tf_op jit(solution)/shard_map/all_to_all | solution.py:92
  563.6 29.2 %gather_fusion.8 = bf16[8192,128]{1,0:T(8,128)(2,1)} fusion(bf16[12288,128]{1,0:T(8,128)(2,1)S(1)} %bitcast.77, s32[8192]{0:T(1024)S(1)} %fusion.67), kind=kCustom, calls=%fused_computation.8 | custom fusion | bytes 4227072 | tf_op jit(solution)/shard_map/gather | solution.py:93
  592.8 4.2 copy.28
  597.1 3.4 add_convert_fusion
  600.5 4.1 copy.29
  (66 shorter events, 0.6 us)
Async XLA Ops:
  4.9 26.8 %all-to-all-start = ((bf16[8,64,128]{2,1,0:T(8,128)(2,1)}), bf16[8,64,128]{2,1,0:T(8,128)(2,1)S(1)}, u32[]{:S(2)}, u32[]{:S(2)}) async-start(bf16[8,64,128]{2,1,0:T(8,128)(2,1)} %bitcast.1), calls=%async_computation | async-start | bytes 262144 | tf_op jit(solution)/shard_map/all_to_all | solution.py:28
  13.7 5.8 copy-start
  19.5 12.1 %copy-start.8 = (s32[4096]{0:T(1024)S(1)}, s32[4096]{0:T(1024)}, u32[]{:S(2)}) copy-start(s32[4096]{0:T(1024)} %param.20) | copy-start | bytes 49156
  37.3 16.2 %copy-start.15 = (bf16[2,128,128]{2,1,0:T(8,128)(2,1)S(1)}, bf16[2,128,128]{2,1,0:T(8,128)(2,1)}, u32[]{:S(2)}) copy-start(bf16[2,128,128]{2,1,0:T(8,128)(2,1)} %param.31) | copy-start | bytes 196612
  57.8 2.2 copy-start.4
  89.4 77.1 %copy-start.14 = (bf16[2,256,128]{2,1,0:T(8,128)(2,1)S(1)}, bf16[2,256,128]{2,1,0:T(8,128)(2,1)}, u32[]{:S(2)}) copy-start(bf16[2,256,128]{2,1,0:T(8,128)(2,1)} %param.32) | copy-start | bytes 393220
  89.4 77.1 %copy-start.17 = (bf16[2,128,128]{2,1,0:T(8,128)(2,1)S(1)}, bf16[2,128,128]{2,1,0:T(8,128)(2,1)}, u32[]{:S(2)}) copy-start(bf16[2,128,128]{2,1,0:T(8,128)(2,1)} %param.33) | copy-start | bytes 196612
  172.3 3.4 copy-start.2
  226.0 5.5 copy-start.6
  226.0 5.5 copy-start.9
  226.0 81.0 %copy-start.10 = (s32[1024]{0:T(1024)S(1)}, s32[1024]{0:T(1024)}, u32[]{:S(2)}) copy-start(s32[1024]{0:T(1024)} %param.24) | copy-start | bytes 12292
  226.0 81.0 %all-to-all-start.1 = ((bf16[8,1536,128]{2,1,0:T(8,128)(2,1)}), bf16[8,1536,128]{2,1,0:T(8,128)(2,1)S(1)}, u32[]{:S(2)}, u32[]{:S(2)}) async-start(bf16[8,1536,128]{2,1,0:T(8,128)(2,1)} %bitcast.79), calls=%async_computation.1 | async-start | bytes 6291456 | tf_op jit(solution)/shard_map/all_to_all | solution.py:86
  307.0 91.4 %copy-start.11 = (s32[1024]{0:T(1024)S(1)}, s32[1024]{0:T(1024)}, u32[]{:S(2)}) copy-start(s32[1024]{0:T(1024)} %param.25) | copy-start | bytes 12292
  386.8 18.5 %all-to-all-start.2 = ((bf16[8,32,128]{2,1,0:T(8,128)(2,1)}), bf16[8,32,128]{2,1,0:T(8,128)(2,1)S(1)}, u32[]{:S(2)}, u32[]{:S(2)}) async-start(bf16[8,32,128]{2,1,0:T(8,128)(2,1)} %bitcast.13), calls=%async_computation.2 | async-start | bytes 131072 | tf_op jit(solution)/shard_map/all_to_all | solution.py:28
  401.7 6.9 %copy-start.12 = (bf16[1024,128]{1,0:T(8,128)(2,1)S(1)}, bf16[1024,128]{1,0:T(8,128)(2,1)}, u32[]{:S(2)}) copy-start(bf16[1024,128]{1,0:T(8,128)(2,1)} %param.23) | copy-start | bytes 786436
  401.7 6.9 %copy-start.13 = (bf16[2,384,128]{2,1,0:T(8,128)(2,1)S(1)}, bf16[2,384,128]{2,1,0:T(8,128)(2,1)}, u32[]{:S(2)}) copy-start(bf16[2,384,128]{2,1,0:T(8,128)(2,1)} %param.30) | copy-start | bytes 589828
  401.7 6.9 %copy-start.16 = (bf16[2,128,128]{2,1,0:T(8,128)(2,1)S(1)}, bf16[2,128,128]{2,1,0:T(8,128)(2,1)}, u32[]{:S(2)}) copy-start(bf16[2,128,128]{2,1,0:T(8,128)(2,1)} %param.31) | copy-start | bytes 196612
  409.5 32.3 %copy-start.18 = (bf16[2,128,128]{2,1,0:T(8,128)(2,1)S(1)}, bf16[2,128,128]{2,1,0:T(8,128)(2,1)}, u32[]{:S(2)}) copy-start(bf16[2,128,128]{2,1,0:T(8,128)(2,1)} %param.33) | copy-start | bytes 196612
  441.8 1.5 copy-start.3
  444.3 0.8 copy-start.5
  488.5 3.8 copy-start.7
  488.5 75.1 %all-to-all-start.3 = ((bf16[8,1536,128]{2,1,0:T(8,128)(2,1)}), bf16[8,1536,128]{2,1,0:T(8,128)(2,1)S(1)}, u32[]{:S(2)}, u32[]{:S(2)}) async-start(bf16[8,1536,128]{2,1,0:T(8,128)(2,1)} %bitcast.80), calls=%async_computation.3 | async-start | bytes 6291456 | tf_op jit(solution)/shard_map/all_to_all | solution.py:92
  592.8 4.2 copy-start.1
where the time goes:
time: 606 us; the launch traced here: 605 us
  other arithmetic  208 us (34%)
  local copies, waits for them, and re-layouts  178 us (29%)
  blocking collectives  103 us (17%)
  waiting for transfers between devices  74.9 us (12%)
  starting transfers between devices  28.2 us (5%)
  matrix products  11.6 us (2%)
    psum x2, blocking collectives, graph_layer(): summed = lax.psum(partial_sum, 'edge')  103 us
    scatter-add x1, other arithmetic, pooled_mean(): jax.ops.segment_sum(arrived.reshape(-1, width).astype(jnp.float32), place...  76.8 us
    scatter-add x1, other arithmetic, pooled_mean(): jax.ops.segment_sum(jnp.ones_like(places), places, num_segments=COARSE + 1)  75.2 us
    all_to_all x1, waiting for transfers between devices, shards(): lax.all_to_all(padded[pool_dest[0]], 'dom', split_axis=0, concat_axis=0,...  71.3 us
    gather x1, local copies, waits for them, and re-layouts, shards(): padded[pool_dest[0]]  43.3 us
    gather x1, local copies, waits for them, and re-layouts, shards(): fine_mid[pool_send[0]]  43.3 us
    gather x4, local copies, waits for them, and re-layouts, graph_layer(): inputs = jnp.concatenate([table[senders], nodes[receivers], edges], axis=1)  34.7 us
    gather x2, local copies, waits for them, and re-layouts, shards(): parents = back.reshape(-1, width)[unpool_slot]  33.5 us
  transfers between devices with their start and end apart: 4, of which 2 were waited for; matrix products, arithmetic and copies ran while one was open for 16% of the time, Pallas kernels for 0%

commit v1 on v0

--- a/solution.py
+++ b/solution.py
@@ -36,7 +36,7 @@
         edge_gain[level],
     )
     partial_sum = jax.ops.segment_sum(message, receivers, num_segments=nodes.shape[0])
-    summed = lax.psum(partial_sum, "edge")
+    summed = jnp.sum(lax.all_gather(partial_sum, "edge"), axis=0)
     return node_update(
         nodes, summed, node_in_weight[level], node_out_weight[level], node_gain[level]
     )

time: 606 us -> 665 us (1.097)
  waiting for transfers between devices: 74.9 us -> 210 us
  blocking collectives: 103 us -> 0 us
  between operations: 1.07 us -> 14.5 us
  other arithmetic: 208 us -> 219 us
    all_gather x0 -> x2, waiting for transfers between devices: none -> 136 us  [graph_layer(): summed = jnp.sum(lax.all_gather(partial_sum, 'edge'), axis=0)]
    psum x2 -> x0, blocking collectives: 103 us -> none  [graph_layer(): summed = lax.psum(partial_sum, 'edge')]
    reduce_sum x0 -> x2, other arithmetic: none -> 11.2 us  [graph_layer(): summed = jnp.sum(lax.all_gather(partial_sum, 'edge'), axis=0)]
  transfers between devices with their start and end apart: 4 -> 6, of which waited for: 2 -> 4; matrix products, arithmetic and copies ran while one was open for 16% -> 14% of each run, Pallas kernels for 0% -> 0%
where the time goes in v1:
time: 665 us; the launch traced here: 664 us
  other arithmetic  219 us (33%)
  waiting for transfers between devices  210 us (32%)
  local copies, waits for them, and re-layouts  178 us (27%)
  starting transfers between devices  30.5 us (5%)
  between operations  14.5 us (2%)
  matrix products  11.5 us (2%)
    all_gather x2, waiting for transfers between devices, graph_layer(): summed = jnp.sum(lax.all_gather(partial_sum, 'edge'), axis=0)  136 us
    scatter-add x1, other arithmetic, pooled_mean(): jax.ops.segment_sum(arrived.reshape(-1, width).astype(jnp.float32), place...  76.7 us
    scatter-add x1, other arithmetic, pooled_mean(): jax.ops.segment_sum(jnp.ones_like(places), places, num_segments=COARSE + 1)  75.2 us
    all_to_all x1, waiting for transfers between devices, shards(): lax.all_to_all(padded[pool_dest[0]], 'dom', split_axis=0, concat_axis=0,...  71.1 us
    gather x1, local copies, waits for them, and re-layouts, shards(): padded[pool_dest[0]]  43.6 us
    gather x1, local copies, waits for them, and re-layouts, shards(): fine_mid[pool_send[0]]  43.6 us
    gather x4, local copies, waits for them, and re-layouts, graph_layer(): inputs = jnp.concatenate([table[senders], nodes[receivers], edges], axis=1)  35.7 us
    gather x2, local copies, waits for them, and re-layouts, shards(): parents = back.reshape(-1, width)[unpool_slot]  33.7 us
  transfers between devices with their start and end apart: 6, of which 4 were waited for; matrix products, arithmetic and copies ran while one was open for 14% of the time, Pallas kernels for 0%

profile of v1, /device:TPU:0, one launch (start us, length us, event | category | flops | bytes accessed | tf_op | source)
XLA Modules:
  0.0 663.7 jit_solution(4371880036239416877)
XLA Ops:
  7.2 0.7 compare_select_fusion.8
  7.9 3.5 gather_fusion
  11.5 7.3 %all-to-all-start = ((bf16[8,64,128]{2,1,0:T(8,128)(2,1)}), bf16[8,64,128]{2,1,0:T(8,128)(2,1)S(1)}, u32[]{:S(2)}, u32[]{:S(2)}) async-start(bf16[8,64,128]{2,1,0:T(8,128)(2,1)} %bitcast.1), calls=%async_computation | async-start | bytes 262144 | tf_op jit(solution)/shard_map/all_to_all | solution.py:28
  18.8 0.7 fusion.77
  19.5 0.8 slice_bitcast_fusion.1
  20.3 13.0 %gather_fusion.2 = bf16[4096,128]{1,0:T(8,128)(2,1)S(1)} fusion(bf16[8192,128]{1,0:T(8,128)(2,1)} %param.18, s32[4096]{0:T(1024)S(1)} %fusion.77), kind=kCustom, calls=%fused_computation.2 | custom fusion | bytes 2113536 | tf_op jit(solution)/shard_map/gather | solution.py:30
  33.4 5.6 pad_maximum_fusion
  39.0 16.3 %gather_fusion.1 = bf16[4096,128]{1,0:T(8,128)(2,1)} fusion(bf16[8704,128]{1,0:T(8,128)(2,1)} %pad_maximum_fusion, s32[4096]{0:T(1024)S(1)} %fusion.76), kind=kCustom, calls=%fused_computation.1 | custom fusion | bytes 2113536 | tf_op jit(solution)/shard_map/gather | solution.py:30
  55.2 4.3 fusion.95
  59.5 2.0 multiply_reduce_fusion.1
  61.5 0.2 copy-done.4
  61.7 1.6 multiply_multiply_fusion
  63.4 2.9 copy.25
  66.3 24.8 %scatter_custom_fusion = f32[8192,128]{1,0:T(8,128)} fusion(s32[4096]{0:T(1024)} %param.21, f32[4096,128]{1,0:T(8,128)} %copy.25, f32[]{:T(128)} %constant.13.clone.1), kind=kCustom, calls=%fused_computation.33 | custom fusion | flops 524288 | bytes 4194816 | tf_op jit(solution)/shard_map/scatter-add | solution.py:38
  91.2 2.9 copy.24
  94.1 104.4 %all-gather.5.cloned.1.call-done = f32[32768,128]{1,0:T(8,128)} async-done(((f32[8192,128]{1,0:T(8,128)}), f32[32768,128]{1,0:T(8,128)}) %all-gather.5.cloned.1.call-update) | async-done | bytes 16777232 | tf_op jit(solution)/shard_map/all_gather | solution.py:39
  198.6 8.7 %reduce_sum.92 = bf16[8192,128]{1,0:T(8,128)(2,1)} reduce(f32[4,8192,128]{2,1,0:T(8,128)} %bitcast.80, f32[]{:T(128)} %constant.13.clone.1), dimensions={0}, to_apply=%region_3.4 | reduce | flops 3145728 | bytes 18874372 | tf_op jit(solution)/shard_map/reduce_sum | solution.py:39
  207.3 5.8 fusion.100
  213.1 2.8 multiply_reduce_fusion
  215.9 0.6 copy-done.2
  216.5 3.8 add_convert_fusion.1
  220.3 3.2 copy.26
  223.5 43.6 %gather_fusion.3 = bf16[12288,128]{1,0:T(8,128)(2,1)} fusion(bf16[8192,128]{1,0:T(8,128)(2,1)S(1)} %copy.26, s32[12288]{0:T(1024)S(1)} %broadcast_clamp_fusion.1), kind=kCustom, calls=%fused_computation.3 | custom fusion | bytes 6340608 | tf_op jit(solution)/shard_map/gather | solution.py:86
  267.2 5.7 all-to-all-start.1
  272.9 75.2 %scatter_custom_fusion.2 = s32[2049]{0:T(1024)S(1)} fusion(s32[12288]{0:T(1024)S(1)} %reshape.263, s32[12288]{0:T(1024)S(1)} %broadcast.163, s32[]{:T(128)} %constant.14.clone.1), kind=kCustom, calls=%fused_computation.101 | custom fusion | flops 12288 | bytes 8200 | tf_op jit(solution)/shard_map/scatter-add | solution.py:49
  348.3 76.7 %scatter_custom_fusion.1 = f32[2049,128]{1,0:T(8,128)} fusion(s32[12288]{0:T(1024)S(1)} %reshape.263, bf16[12288,128]{1,0:T(8,128)(2,1)S(1)} %bitcast.81, f32[]{:T(128)} %constant.13.clone.1), kind=kCustom, calls=%fused_computation.13 | custom fusion | flops 3145728 | bytes 4194820 | tf_op jit(solution)/shard_map/scatter-add | solution.py:46
  425.0 1.6 fusion.24
  426.6 1.5 gather_fusion.4
  428.0 11.6 %all-to-all-start.2 = ((bf16[8,32,128]{2,1,0:T(8,128)(2,1)}), bf16[8,32,128]{2,1,0:T(8,128)(2,1)S(1)}, u32[]{:S(2)}, u32[]{:S(2)}) async-start(bf16[8,32,128]{2,1,0:T(8,128)(2,1)} %bitcast.14), calls=%async_computation.2 | async-start | bytes 131072 | tf_op jit(solution)/shard_map/all_to_all | solution.py:28
  439.7 0.3 all-gather.7.cloned.1.call-start
  440.0 3.2 gather_fusion.6
  443.2 3.4 all-to-all-done.2
  446.6 3.2 gather_fusion.5
  449.9 0.6 fusion.105
  450.9 7.0 %scatter_custom_fusion.3 = f32[2048,128]{1,0:T(8,128)} fusion(s32[1024]{0:T(1024)S(1)} %copy-done.12, f32[1024,128]{1,0:T(8,128)S(1)} %copy.27, f32[]{:T(128)} %constant.13.clone.1), kind=kCustom, calls=%fused_computation.61 | custom fusion | flops 131072 | bytes 1048580 | tf_op jit(solution)/shard_map/scatter-add | solution.py:38
  458.0 31.4 %all-gather.7.cloned.1.call-done = f32[8192,128]{1,0:T(8,128)} async-done(((f32[2048,128]{1,0:T(8,128)}), f32[8192,128]{1,0:T(8,128)}) %all-gather.7.cloned.1.call-update) | async-done | bytes 4194320 | tf_op jit(solution)/shard_map/all_gather | solution.py:39
  489.4 2.5 reduce_sum.97
  491.9 0.9 fusion.110
  492.8 0.6 multiply_reduce_fusion.2
  493.5 1.0 add_convert_fusion.2
  494.5 0.8 copy-done.5
  495.3 43.6 %gather_fusion.7 = bf16[12288,128]{1,0:T(8,128)(2,1)} fusion(bf16[2049,128]{1,0:T(8,128)(2,1)S(1)} %concatenate.27, s32[12288]{0:T(1024)S(1)} %broadcast_clamp_fusion), kind=kCustom, calls=%fused_computation.7 | custom fusion | bytes 6340608 | tf_op jit(solution)/shard_map/gather | solution.py:92
  539.0 5.6 all-to-all-start.3
  544.6 71.1 %all-to-all-done.3 = bf16[8,1536,128]{2,1,0:T(8,128)(2,1)S(1)} async-done(((bf16[8,1536,128]{2,1,0:T(8,128)(2,1)}), bf16[8,1536,128]{2,1,0:T(8,128)(2,1)S(1)}, u32[]{:S(2)}, u32[]{:S(2)}) %all-to-all-start.3) | async-done | bytes 3145760 | tf_op jit(solution)/shard_map/all_to_all | solution.py:92
  615.7 29.4 %gather_fusion.8 = bf16[8192,128]{1,0:T(8,128)(2,1)} fusion(bf16[12288,128]{1,0:T(8,128)(2,1)S(1)} %bitcast.79, s32[8192]{0:T(1024)S(1)} %fusion.67), kind=kCustom, calls=%fused_computation.8 | custom fusion | bytes 4227072 | tf_op jit(solution)/shard_map/gather | solution.py:93
  645.1 4.2 copy.28
  649.4 3.4 add_convert_fusion
  652.8 4.1 copy.29
  (78 shorter events, 0.9 us)
Async XLA Ops:
  11.5 21.9 %all-to-all-start = ((bf16[8,64,128]{2,1,0:T(8,128)(2,1)}), bf16[8,64,128]{2,1,0:T(8,128)(2,1)S(1)}, u32[]{:S(2)}, u32[]{:S(2)}) async-start(bf16[8,64,128]{2,1,0:T(8,128)(2,1)} %bitcast.1), calls=%async_computation | async-start | bytes 262144 | tf_op jit(solution)/shard_map/all_to_all | solution.py:28
  18.8 179.8 %all-gather.5.cloned.1.call-start = ((), (), s32[]{:S(2)}) async-start(), calls=%async_computation.4 | async-start | bytes 20971520 | tf_op jit(solution)/shard_map/all_gather | solution.py:39
  20.3 13.0 %copy-start.9 = (s32[4096]{0:T(1024)S(1)}, s32[4096]{0:T(1024)}, u32[]{:S(2)}) copy-start(s32[4096]{0:T(1024)} %param.20) | copy-start | bytes 49156
  20.3 13.1 %copy-start = (bf16[8192,128]{1,0:T(8,128)(2,1)S(1)}, bf16[8192,128]{1,0:T(8,128)(2,1)}, u32[]{:S(2)}) copy-start(bf16[8192,128]{1,0:T(8,128)(2,1)} %param.18) | copy-start | bytes 6291460
  39.0 16.3 %copy-start.15 = (bf16[2,384,128]{2,1,0:T(8,128)(2,1)S(1)}, bf16[2,384,128]{2,1,0:T(8,128)(2,1)}, u32[]{:S(2)}) copy-start(bf16[2,384,128]{2,1,0:T(8,128)(2,1)} %param.30) | copy-start | bytes 589828
  39.0 16.3 %copy-start.18 = (bf16[2,128,128]{2,1,0:T(8,128)(2,1)S(1)}, bf16[2,128,128]{2,1,0:T(8,128)(2,1)}, u32[]{:S(2)}) copy-start(bf16[2,128,128]{2,1,0:T(8,128)(2,1)} %param.31) | copy-start | bytes 196612
  59.5 2.2 copy-start.4
  91.1 2.9 copy-start.7
  91.1 2.9 copy-start.13
  198.6 8.7 %copy-start.16 = (bf16[2,256,128]{2,1,0:T(8,128)(2,1)S(1)}, bf16[2,256,128]{2,1,0:T(8,128)(2,1)}, u32[]{:S(2)}) copy-start(bf16[2,256,128]{2,1,0:T(8,128)(2,1)} %param.32) | copy-start | bytes 393220
  198.6 8.7 %copy-start.20 = (bf16[2,128,128]{2,1,0:T(8,128)(2,1)S(1)}, bf16[2,128,128]{2,1,0:T(8,128)(2,1)}, u32[]{:S(2)}) copy-start(bf16[2,128,128]{2,1,0:T(8,128)(2,1)} %param.33) | copy-start | bytes 196612
  213.1 3.4 copy-start.2
  267.1 5.7 copy-start.6
  267.2 5.7 copy-start.10
  267.2 81.1 %copy-start.11 = (s32[1024]{0:T(1024)S(1)}, s32[1024]{0:T(1024)}, u32[]{:S(2)}) copy-start(s32[1024]{0:T(1024)} %param.24) | copy-start | bytes 12292
  267.2 81.1 %all-to-all-start.1 = ((bf16[8,1536,128]{2,1,0:T(8,128)(2,1)}), bf16[8,1536,128]{2,1,0:T(8,128)(2,1)S(1)}, u32[]{:S(2)}, u32[]{:S(2)}) async-start(bf16[8,1536,128]{2,1,0:T(8,128)(2,1)} %bitcast.82), calls=%async_computation.1 | async-start | bytes 6291456 | tf_op jit(solution)/shard_map/all_to_all | solution.py:86
  348.2 91.7 %copy-start.12 = (s32[1024]{0:T(1024)S(1)}, s32[1024]{0:T(1024)}, u32[]{:S(2)}) copy-start(s32[1024]{0:T(1024)} %param.25) | copy-start | bytes 12292
  428.0 18.5 %all-to-all-start.2 = ((bf16[8,32,128]{2,1,0:T(8,128)(2,1)}), bf16[8,32,128]{2,1,0:T(8,128)(2,1)S(1)}, u32[]{:S(2)}, u32[]{:S(2)}) async-start(bf16[8,32,128]{2,1,0:T(8,128)(2,1)} %bitcast.14), calls=%async_computation.2 | async-start | bytes 131072 | tf_op jit(solution)/shard_map/all_to_all | solution.py:28
  439.7 49.7 %all-gather.7.cloned.1.call-start = ((), (), s32[]{:S(2)}) async-start(), calls=%async_computation.5 | async-start | bytes 5242880 | tf_op jit(solution)/shard_map/all_gather | solution.py:39
  443.2 6.7 %copy-start.14 = (bf16[1024,128]{1,0:T(8,128)(2,1)S(1)}, bf16[1024,128]{1,0:T(8,128)(2,1)}, u32[]{:S(2)}) copy-start(bf16[1024,128]{1,0:T(8,128)(2,1)} %param.23) | copy-start | bytes 786436
  443.2 6.7 %copy-start.19 = (bf16[2,128,128]{2,1,0:T(8,128)(2,1)S(1)}, bf16[2,128,128]{2,1,0:T(8,128)(2,1)}, u32[]{:S(2)}) copy-start(bf16[2,128,128]{2,1,0:T(8,128)(2,1)} %param.31) | copy-start | bytes 196612
  489.4 2.5 copy-start.17
  489.4 2.5 copy-start.21
  491.9 1.5 copy-start.3
  494.5 0.8 copy-start.5
  539.0 5.7 copy-start.8
  539.0 76.8 %all-to-all-start.3 = ((bf16[8,1536,128]{2,1,0:T(8,128)(2,1)}), bf16[8,1536,128]{2,1,0:T(8,128)(2,1)S(1)}, u32[]{:S(2)}, u32[]{:S(2)}) async-start(bf16[8,1536,128]{2,1,0:T(8,128)(2,1)} %bitcast.83), calls=%async_computation.3 | async-start | bytes 6291456 | tf_op jit(solution)/shard_map/all_to_all | solution.py:92
  645.1 4.3 copy-start.1
Sparse Core Ops, SparseCore 0:
  91.3 107.2 all-gather.4
  458.1 31.3 all-gather.6
